TPU v7x, 512 devices: a whole 4x8x8 slice. The times are simulated.
512 devices in a mesh: gx: 4 (over y_lo), gy: 16 (over y_hi, z), gz: 8 (over x, core).
Axes of the slice: x: 4, y: 8 (y_hi: 2, y_lo: 4; y = y_hi * 4 + y_lo), z: 8, core: 2. Of those that a mesh axis runs over, the one named last changes fastest.
Arguments:
- grads: float32 [4, 16, 8, 160, 4096], P('gx', 'gy', 'gz'), may hold values from -6 to 6
- peer_table: int32 [16], replicated, may hold values from 0 to 15, each once
- layer_offsets: int32 [2], replicated, may hold values from 0 to 96, as said below
Outputs:
- averaged: float32 [4, 16, 8, 128, 4096], P('gx', 'gy', 'gz')
Inputs may be any that keep to these rules, and one draw needn't show every extreme that they name: layer_offsets[l] is a multiple of 8 between l * (80) and l * 80 + 16; the last layer's offset is the largest of these.
All inputs are finite; a program needn't handle non-finite values.
Results may differ from a plain program's by a relative error of at most 0.00002.
Values sent between devices are 32-bit elements; how exact they have to be, the bound alone decides.
No kernel may reach another device: no remote copies, remote signals or barrier semaphores. Data moves between devices by JAX's collectives and lax.ppermute only.
A program may use at most 64 MiB of HBM per device.

v0:
```python
import jax
import jax.numpy as jnp
from jax import lax
from jax.sharding import PartitionSpec as P

ROWS = 64
LAYERS = 2


def filled_up(lines, peers):
    spare = -lines.shape[0] % peers
    if not spare:
        return lines
    return jnp.concatenate([lines, jnp.zeros((spare, *lines.shape[1:]), lines.dtype)])


def sum_by_parts(shard, axis):
    lines = shard.reshape(-1, *shard.shape[1:][-1:])
    own = lax.psum_scatter(
        filled_up(lines, lax.axis_size(axis)), axis, scatter_dimension=0, tiled=True
    )
    whole = lax.all_gather(own, axis).reshape(-1, *lines.shape[1:])
    return lax.slice_in_dim(whole, 0, len(lines)).reshape(shard.shape)


def on_device(grads, peer_table, layer_offsets):
    buffer = grads[0, 0, 0]
    pieces = [lax.dynamic_slice_in_dim(buffer, layer_offsets[i], ROWS, 0) for i in range(LAYERS)]
    packed = jnp.concatenate(pieces, axis=0)
    count_y = lax.axis_size("gy")
    group_b = min(8, count_y)
    group_a = lax.axis_size("gx") * (count_y // group_b)
    places = jnp.arange(count_y, dtype=jnp.int32)
    onehot = (peer_table[:, None] == places[None, :]).astype(jnp.int32)
    inverse = jnp.sum(onehot * places[:, None], axis=0)
    spread = lax.all_to_all(packed[None], "gy", split_axis=1, concat_axis=0, tiled=True)
    current = jnp.take(spread, peer_table, axis=0)
    total_c = sum_by_parts(current, "gz")
    current = 0.5 * current + 0.5 / lax.axis_size("gz") * total_c
    block_rows = current.shape[1]
    width = current.shape[2]
    split = current.reshape(count_y // group_b, group_b, block_rows, width)
    total_b = jnp.sum(split, axis=1, keepdims=True)
    split = 0.5 * split + 0.5 / group_b * total_b
    local_a = jnp.sum(split, axis=0, keepdims=True)
    total_a = lax.psum(local_a, "gx")
    split = 0.5 * split + 0.5 / group_a * total_a
    current = jnp.take(split.reshape(count_y, block_rows, width), inverse, axis=0)
    result = lax.all_to_all(current, "gy", split_axis=0, concat_axis=1, tiled=True)[0]
    return result[None, None, None]


def solution(mesh):
    placed = (P("gx", "gy", "gz", None, None), P(), P())
    return jax.shard_map(
        on_device,
        mesh=mesh,
        in_specs=placed,
        out_specs=P("gx", "gy", "gz", None, None),
        check_vma=False,
    )
```

profile of v0, /device:TPU:8, one launch (start us, length us, event | category | flops | bytes accessed | tf_op | source)
XLA Modules:
  0.0 328.4 jit_solution(8673940467536958085)
XLA Ops:
  6.5 1.4 fusion.2
  11.8 1.8 dynamic-slice_bitcast_fusion.1
  13.6 0.1 pad_maximum_fusion
  13.7 3.7 %broadcast_in_dim.19 = f32[1,128,4096]{2,0,1:T(1,128)} reshape(f32[128,4096]{1,0:T(8,128)S(1)} %pad_maximum_fusion) | data formatting | bytes 4194304 | tf_op jit(solution)/shard_map/broadcast_in_dim | solution.py:36
  17.4 0.0 copy-start.2
  17.4 14.9 %all-to-all-start = ((f32[1,128,4096]{2,0,1:T(1,128)}), f32[1,128,4096]{2,0,1:T(1,128)S(1)}, u32[]{:S(2)}, u32[]{:S(2)}) async-start(f32[1,128,4096]{2,0,1:T(1,128)} %broadcast_in_dim.19), calls=%async_computation | async-start | bytes 4194304 | tf_op jit(solution)/shard_map/all_to_all | solution.py:36
  32.4 0.0 reduce-scatter.2.cloned.1.call-start
  32.4 0.0 copy-done.2
  32.5 57.0 %all-to-all-done = f32[1,128,4096]{2,0,1:T(1,128)S(1)} async-done(((f32[1,128,4096]{2,0,1:T(1,128)}), f32[1,128,4096]{2,0,1:T(1,128)S(1)}, u32[]{:S(2)}, u32[]{:S(2)}) %all-to-all-start) | async-done | bytes 2097184 | tf_op jit(solution)/shard_map/all_to_all | solution.py:36
  89.5 3.0 copy.6
  92.4 2.3 gather_fusion
  94.7 1.6 select_bitcast_fusion
  96.3 0.0 reduce-scatter.2.cloned.1.call-update
  96.3 0.0 all-gather.3.cloned.1.call-start
  96.4 48.3 %reduce-scatter.2.cloned.1.call-done = f32[16,4096]{1,0:T(8,128)} async-done(((f32[128,4096]{1,0:T(8,128)}), f32[16,4096]{1,0:T(8,128)}) %reduce-scatter.2.cloned.1.call-update) | async-done | bytes 262160 | tf_op jit(solution)/shard_map/reduce_scatter | solution.py:19
  144.7 0.0 all-gather.3.cloned.1.call-update
  144.7 0.0 all-reduce.2.cloned.1.call-start
  144.7 31.6 %all-gather.3.cloned.1.call-done = f32[128,4096]{1,0:T(8,128)} async-done(((f32[16,4096]{1,0:T(8,128)}), f32[128,4096]{1,0:T(8,128)}) %all-gather.3.cloned.1.call-update) | async-done | bytes 2097168 | tf_op jit(solution)/shard_map/all_gather | solution.py:22
  176.4 2.1 bitcast_reduce_fusion
  178.5 0.0 copy-start
  178.5 1.3 copy-done
  179.8 0.2 fusion.1
  180.0 1.2 reduce_sum.28
  181.3 0.0 copy-start.1
  181.3 0.0 all-reduce.2.cloned.1.call-update
  181.3 0.1 select_reduce_fusion
  181.4 68.4 %all-reduce.2.cloned.1.call-done = f32[1,8,8,4096]{3,2,1,0:T(8,128)} async-done(((f32[1,8,8,4096]{3,2,1,0:T(8,128)}), f32[1,8,8,4096]{3,2,1,0:T(8,128)}) %all-reduce.2.cloned.1.call-update) | async-done | bytes 1048592 | tf_op jit(solution)/shard_map/psum | solution.py:46
  249.8 1.3 multiply_bitcast_fusion
  251.1 0.0 copy-done.1
  251.1 1.6 bitcast_add_fusion
  252.7 2.3 gather_fusion.1
  255.0 0.3 broadcast_select_fusion
  255.2 65.4 %all_to_all.21 = f32[16,8,4096]{2,1,0:T(8,128)S(1)} all-to-all(f32[16,8,4096]{2,1,0:T(8,128)S(1)} %broadcast_select_fusion), channel_id=1, replica_groups=mesh['gx'=4,'gy'=16,'gz'=8] {'gy'}, dimensions={0} | all-to-all | bytes 4194304 | tf_op jit(solution)/shard_map/all_to_all | solution.py:49
  320.6 1.3 copy.9
  (7 shorter events, 0.1 us)
Async XLA Ops:
  17.4 15.0 %copy-start.2 = (s32[16]{0:T(128)S(1)}, s32[16]{0:T(128)}, u32[]{:S(2)}) copy-start(s32[16]{0:T(128)} %param.6) | copy-start | bytes 196
  17.4 72.0 %all-to-all-start = ((f32[1,128,4096]{2,0,1:T(1,128)}), f32[1,128,4096]{2,0,1:T(1,128)S(1)}, u32[]{:S(2)}, u32[]{:S(2)}) async-start(f32[1,128,4096]{2,0,1:T(1,128)} %broadcast_in_dim.19), calls=%async_computation | async-start | bytes 4194304 | tf_op jit(solution)/shard_map/all_to_all | solution.py:36
  32.4 112.3 %reduce-scatter.2.cloned.1.call-start = ((), (), s32[]{:S(2)}) async-start(), calls=%async_computation.3 | async-start | bytes 2359296 | tf_op jit(solution)/shard_map/reduce_scatter | solution.py:19
  96.3 80.1 %all-gather.3.cloned.1.call-start = ((), (), s32[]{:S(2)}) async-start(), calls=%async_computation.5 | async-start | bytes 2359296 | tf_op jit(solution)/shard_map/all_gather | solution.py:22
  144.7 105.1 %all-reduce.2.cloned.1.call-start = ((), (), s32[]{:S(2)}) async-start(), calls=%async_computation.4 | async-start | bytes 2097152 | tf_op jit(solution)/shard_map/psum | solution.py:46
  178.5 1.3 copy-start
  181.3 69.8 %copy-start.1 = (f32[16,8,4096]{2,1,0:T(8,128)S(1)}, f32[16,8,4096]{2,1,0:T(8,128)}, u32[]{:S(2)}) copy-start(f32[16,8,4096]{2,1,0:T(8,128)} %copy-done) | copy-start | bytes 6291460
Sparse Core Ops, SparseCore 0:
  96.4 48.1 reduce-scatter.1
  146.8 29.5 all-gather.2
  181.4 68.3 all-reduce.1
where the time goes:
time: 329 us; the launch traced here: 328 us
  waiting for transfers between devices  205 us (62%)
  blocking collectives  65.4 us (20%)
  between operations  17.1 us (5%)
  local copies, waits for them, and re-layouts  17 us (5%)
  starting transfers between devices  15 us (5%)
  other arithmetic  8.57 us (3%)
    psum x1, waiting for transfers between devices, on_device(): total_a = lax.psum(local_a, 'gx')  68.4 us
    all_to_all x1, blocking collectives, on_device(): lax.all_to_all(current, 'gy', split_axis=0, concat_axis=1, tiled=True)[0]  65.4 us
    all_to_all x1, waiting for transfers between devices, on_device(): lax.all_to_all(packed[None], 'gy', split_axis=1, concat_axis=0, tiled=True)  57 us
    reduce_scatter x1, waiting for transfers between devices, sum_by_parts(): lax.psum_scatter(filled_up(lines, lax.axis_size(axis)), axis, scatter_dim...  48.3 us
    all_gather x1, waiting for transfers between devices, sum_by_parts(): whole = lax.all_gather(own, axis).reshape(-1, *lines.shape[1:])  31.6 us
    all_to_all x1, starting transfers between devices, on_device(): lax.all_to_all(packed[None], 'gy', split_axis=1, concat_axis=0, tiled=True)  14.9 us
  transfers between devices with their start and end apart: 4, of which 4 were waited for; matrix products, arithmetic and copies ran while one was open for 0% of the time, Pallas kernels for 0%

commit v1 on v0

--- a/solution.py
+++ b/solution.py
@@ -43,7 +43,7 @@
     total_b = jnp.sum(split, axis=1, keepdims=True)
     split = 0.5 * split + 0.5 / group_b * total_b
     local_a = jnp.sum(split, axis=0, keepdims=True)
-    total_a = lax.psum(local_a, "gx")
+    total_a = jnp.sum(lax.all_gather(local_a, "gx"), axis=0)
     split = 0.5 * split + 0.5 / group_a * total_a
     current = jnp.take(split.reshape(count_y, block_rows, width), inverse, axis=0)
     result = lax.all_to_all(current, "gy", split_axis=0, concat_axis=1, tiled=True)[0]

time: 329 us -> 349 us (1.061)
  the two profiles are of different devices: /device:TPU:8 before, /device:TPU:16 now
where the time goes in v1:
time: 349 us
  waiting for transfers between devices  225 us (64%)
  blocking collectives  64.3 us (18%)
  local copies, waits for them, and re-layouts  18.2 us (5%)
  between operations  17.1 us (5%)
  starting transfers between devices  14.1 us (4%)
  other arithmetic  10.1 us (3%)
    all_gather x1, waiting for transfers between devices, on_device(): total_a = jnp.sum(lax.all_gather(local_a, 'gx'), axis=0)  87 us
    all_to_all x1, blocking collectives, on_device(): lax.all_to_all(current, 'gy', split_axis=0, concat_axis=1, tiled=True)[0]  64.3 us
    all_to_all x1, waiting for transfers between devices, on_device(): lax.all_to_all(packed[None], 'gy', split_axis=1, concat_axis=0, tiled=True)  60.1 us
    reduce_scatter x1, waiting for transfers between devices, sum_by_parts(): lax.psum_scatter(filled_up(lines, lax.axis_size(axis)), axis, scatter_dim...  46.1 us
    all_gather x1, waiting for transfers between devices, sum_by_parts(): whole = lax.all_gather(own, axis).reshape(-1, *lines.shape[1:])  31.5 us
    all_to_all x1, starting transfers between devices, on_device(): lax.all_to_all(packed[None], 'gy', split_axis=1, concat_axis=0, tiled=True)  14 us
    unnamed x8, local copies, waits for them, and re-layouts  7.06 us
  transfers between devices with their start and end apart: 4, of which 4 were waited for; matrix products, arithmetic and copies ran while one was open for 0% of the time, Pallas kernels for 0%

profile of v1, /device:TPU:16, one launch (start us, length us, event | category | flops | bytes accessed | tf_op | source)
XLA Modules:
  0.0 348.7 jit_solution(8881388975369387660)
XLA Ops:
  6.5 1.4 fusion.2
  11.8 1.8 dynamic-slice_bitcast_fusion.1
  13.6 0.1 pad_maximum_fusion
  13.7 3.7 %broadcast_in_dim.16 = f32[1,128,4096]{2,0,1:T(1,128)} reshape(f32[128,4096]{1,0:T(8,128)S(1)} %pad_maximum_fusion) | data formatting | bytes 4194304 | tf_op jit(solution)/shard_map/broadcast_in_dim | solution.py:36
  17.4 0.0 copy-start.2
  17.4 14.0 %all-to-all-start = ((f32[1,128,4096]{2,0,1:T(1,128)}), f32[1,128,4096]{2,0,1:T(1,128)S(1)}, u32[]{:S(2)}, u32[]{:S(2)}) async-start(f32[1,128,4096]{2,0,1:T(1,128)} %broadcast_in_dim.16), calls=%async_computation | async-start | bytes 4194304 | tf_op jit(solution)/shard_map/all_to_all | solution.py:36
  31.5 0.0 reduce-scatter.2.cloned.1.call-start
  31.5 0.0 copy-done.2
  31.6 60.1 %all-to-all-done = f32[1,128,4096]{2,0,1:T(1,128)S(1)} async-done(((f32[1,128,4096]{2,0,1:T(1,128)}), f32[1,128,4096]{2,0,1:T(1,128)S(1)}, u32[]{:S(2)}, u32[]{:S(2)}) %all-to-all-start) | async-done | bytes 2097184 | tf_op jit(solution)/shard_map/all_to_all | solution.py:36
  91.7 3.0 copy.6
  94.6 2.3 gather_fusion
  96.9 1.6 select_bitcast_fusion
  98.5 0.0 reduce-scatter.2.cloned.1.call-update
  98.5 0.0 all-gather.5.cloned.1.call-start
  98.6 46.1 %reduce-scatter.2.cloned.1.call-done = f32[16,4096]{1,0:T(8,128)} async-done(((f32[128,4096]{1,0:T(8,128)}), f32[16,4096]{1,0:T(8,128)}) %reduce-scatter.2.cloned.1.call-update) | async-done | bytes 262160 | tf_op jit(solution)/shard_map/reduce_scatter | solution.py:19
  144.7 0.0 all-gather.5.cloned.1.call-update
  144.7 0.0 all-gather.7.cloned.1.call-start
  144.7 31.5 %all-gather.5.cloned.1.call-done = f32[128,4096]{1,0:T(8,128)} async-done(((f32[16,4096]{1,0:T(8,128)}), f32[128,4096]{1,0:T(8,128)}) %all-gather.5.cloned.1.call-update) | async-done | bytes 2097168 | tf_op jit(solution)/shard_map/all_gather | solution.py:22
  176.3 2.1 bitcast_reduce_fusion
  178.4 0.0 copy-start
  178.4 1.3 copy-done
  179.7 0.2 fusion.1
  179.9 1.2 reduce_sum.37
  181.1 0.0 all-gather.7.cloned.1.call-update
  181.1 0.1 select_reduce_fusion
  181.3 87.0 %all-gather.7.cloned.1.call-done = f32[32,8,4096]{2,1,0:T(8,128)} async-done(((f32[8,8,4096]{2,1,0:T(8,128)}), f32[32,8,4096]{2,1,0:T(8,128)}) %all-gather.7.cloned.1.call-update) | async-done | bytes 4194320 | tf_op jit(solution)/shard_map/all_gather | solution.py:46
  268.3 2.5 reduce.1
  270.8 0.0 copy-start.1
  270.8 0.1 broadcast_multiply_fusion
  270.9 1.5 copy-done.1
  272.4 0.3 bitcast_add_fusion
  272.7 2.0 gather_fusion.1
  274.7 1.9 broadcast_select_fusion
  276.6 64.3 %all_to_all.21 = f32[16,8,4096]{2,1,0:T(8,128)S(1)} all-to-all(f32[16,8,4096]{2,1,0:T(8,128)S(1)} %broadcast_select_fusion), channel_id=1, replica_groups=mesh['gx'=4,'gy'=16,'gz'=8] {'gy'}, dimensions={0} | all-to-all | bytes 4194304 | tf_op jit(solution)/shard_map/all_to_all | solution.py:49
  340.8 1.3 copy.8
  (7 shorter events, 0.1 us)
Async XLA Ops:
  17.4 14.1 %copy-start.2 = (s32[16]{0:T(128)S(1)}, s32[16]{0:T(128)}, u32[]{:S(2)}) copy-start(s32[16]{0:T(128)} %param.6) | copy-start | bytes 196
  17.4 74.2 %all-to-all-start = ((f32[1,128,4096]{2,0,1:T(1,128)}), f32[1,128,4096]{2,0,1:T(1,128)S(1)}, u32[]{:S(2)}, u32[]{:S(2)}) async-start(f32[1,128,4096]{2,0,1:T(1,128)} %broadcast_in_dim.16), calls=%async_computation | async-start | bytes 4194304 | tf_op jit(solution)/shard_map/all_to_all | solution.py:36
  31.5 113.2 %reduce-scatter.2.cloned.1.call-start = ((), (), s32[]{:S(2)}) async-start(), calls=%async_computation.3 | async-start | bytes 2359296 | tf_op jit(solution)/shard_map/reduce_scatter | solution.py:19
  98.5 77.8 %all-gather.5.cloned.1.call-start = ((), (), s32[]{:S(2)}) async-start(), calls=%async_computation.4 | async-start | bytes 2359296 | tf_op jit(solution)/shard_map/all_gather | solution.py:22
  144.7 123.6 %all-gather.7.cloned.1.call-start = ((), (), s32[]{:S(2)}) async-start(), calls=%async_computation.5 | async-start | bytes 5242880 | tf_op jit(solution)/shard_map/all_gather | solution.py:46
  178.4 1.3 copy-start
  270.8 1.6 copy-start.1
Sparse Core Ops, SparseCore 0:
  98.6 45.9 reduce-scatter.1
  146.8 29.4 all-gather.4
  181.3 86.9 all-gather.6
